TPU v7x, 32 devices: a whole 2x2x4 slice. The times are simulated.
32 devices in a mesh: groups: 2 (over y), dp: 4 (over z), section: 2 (over x), tensor: 2 (over core).
Axes of the slice: x: 2, y: 2, z: 4, core: 2. Of those that a mesh axis runs over, the one named last changes fastest.
Arguments:
- hidden: bfloat16 [128, 8, 5120], P(('groups', 'dp')), parts along dimension 0, may hold values from -6 to 6
- unembed: bfloat16 [128, 8, 5120], P(('groups', 'dp')), parts along dimension 0, may hold values from -0.02734375 to 0.02734375
- value_proj: bfloat16 [2, 5120, 512], P('section', 'dp', 'tensor'), may hold values from -0.078125 to 0.078125
- output_proj: bfloat16 [2, 512, 5120], P('section', 'tensor', 'dp'), may hold values from -0.125 to 0.125
- norm_gains: float32 [2, 5120], P('section'), may hold values from 0.1 to 1.9
- survive: int32 [8], P(('groups', 'dp')), parts along dimension 0, may hold values from 0 to 1, as said below
- lengths: int32 [128], P(('groups', 'dp')), parts along dimension 0, may hold values from 1 to 8
- assign: int32 [128], P(('groups', 'dp')), parts along dimension 0, may hold values from 0 to 16, as said below
- advantage: float32 [128], P(('groups', 'dp')), parts along dimension 0, may hold values from -4 to 4
- reference_logit: float32 [128, 8], P(('groups', 'dp')), parts along dimension 0, may hold values from -4 to 4
- recorded_gap: float32 [128, 8], P(('groups', 'dp')), parts along dimension 0, may hold values from -2 to 2
Outputs:
- grad_value: float32 [4, 5120, 512], P(('groups', 'section'), 'dp', 'tensor'), parts along dimension 0
- grad_output: float32 [4, 512, 5120], P(('groups', 'section'), 'tensor', 'dp'), parts along dimension 0
There are 2 independent parts, one for each index of `groups`. A program takes and returns all parts, laid end to end along the dimension named above; an argument that names none is the same for every part. Nothing has to cross between parts.
Inputs may be any that keep to these rules, and one draw needn't show every extreme that they name: `survive`: 1 where the group of 16 responses is kept, 0 where it is dropped; in every draw all groups of some dp index are kept. `assign`: the 16 slots of a dp index list the local positions (0 to 15) of the responses of its kept groups, each exactly once, then hold 16 in every other slot.
All inputs are finite; a program needn't handle non-finite values.
Results may differ from a plain program's by a relative error of at most 0.029.
Values may be sent and summed in bfloat16 or wider, within the bound.
A program may use at most 64 MiB of HBM per device.

v0:
```python
import math
import jax
import jax.numpy as jnp
from jax import lax
from jax.sharding import PartitionSpec as P

GROUP = 16
MB_RESP = 8
eps_norm = 1e-06
loss_scale = 4096.0
clip_high = math.log(1.28)
clip_low = math.log(0.8)


def from_behind(block, axis, distance):
    devices = range(lax.axis_size(axis))
    route = [(i - distance, i) for i in devices if i - distance in devices]
    return lax.ppermute(block, axis, route)


def norm_forward(row_block, norm_gain):
    values = row_block.astype(jnp.float32)
    inverse = lax.rsqrt(jnp.mean(values * values, axis=-1, keepdims=True) + eps_norm)
    return (values, inverse, (values * inverse * norm_gain).astype(jnp.bfloat16))


def norm_backward(values, inverse, norm_gain, upstream):
    scaled = upstream * norm_gain
    inner_sum = jnp.sum(scaled * values, axis=-1, keepdims=True) / values.shape[-1]
    return inverse * scaled - values * (inverse * inverse * inverse) * inner_sum


def contract_last(left_rows, right_rows):
    return lax.dot_general(
        left_rows, right_rows, (((1,), (1,)), ((), ())), preferred_element_type=jnp.float32
    )


def contract_first(left_rows, right_rows):
    return lax.dot_general(
        left_rows, right_rows, (((0,), (0,)), ((), ())), preferred_element_type=jnp.float32
    )


def take_slot(slot_store, slot_index):
    return lax.dynamic_index_in_dim(slot_store, slot_index, 0, keepdims=False)


def put_slot(slot_store, new_value, slot_index, active):
    previous = take_slot(slot_store, slot_index)
    return lax.dynamic_update_index_in_dim(
        slot_store, jnp.where(active, new_value, previous), slot_index, 0
    )


def local(
    hidden,
    unembed,
    value_proj,
    output_proj,
    norm_gains,
    survive,
    lengths,
    assign,
    advantage,
    reference_logit,
    recorded_gap,
):
    resp_count = hidden.shape[0]
    positions = hidden.shape[1]
    model_width = hidden.shape[2]
    half_value = value_proj.shape[2]
    micro_count = resp_count // MB_RESP
    row_count = MB_RESP * positions
    section_count = lax.axis_size("section")
    section_index = lax.axis_index("section")
    is_last = section_index == section_count - 1
    norm_gain = norm_gains[0]
    alive_mask = jnp.repeat(survive, GROUP)
    local_count = jnp.sum((alive_mask * lengths).astype(jnp.float32))
    gathered_value, gathered_output = (
        lax.all_gather(value_proj, "dp", axis=1, tiled=True),
        lax.all_gather(output_proj, "dp", axis=2, tiled=True),
    )
    w_first = gathered_value[0]
    w_second = gathered_output[0]

    def pick(array):
        return jnp.take(array, assign, axis=0, mode="fill", fill_value=0)

    slot_hidden = pick(hidden).reshape(micro_count, row_count, model_width)
    slot_unembed = pick(unembed).reshape(micro_count, row_count, model_width)
    position_index = lax.broadcasted_iota(jnp.int32, (resp_count, positions), 1)
    live_mask = (position_index < pick(lengths)[:, None]).astype(jnp.float32)
    advantages = jnp.broadcast_to(pick(advantage)[:, None], (resp_count, positions))
    gap_rows = pick(recorded_gap)
    clipped = (advantages > 0) & (gap_rows > clip_high) | (advantages < 0) & (gap_rows < clip_low)
    kept_mask = 1.0 - clipped.astype(jnp.float32)
    weight_rows = (-loss_scale * advantages * kept_mask * live_mask).reshape(micro_count, row_count)
    logit_base = pick(reference_logit).reshape(micro_count, row_count)
    step_count = micro_count + section_count - 1
    store_in = jnp.zeros((micro_count, row_count, model_width), jnp.bfloat16)
    store_normed = jnp.zeros((micro_count, row_count, model_width), jnp.bfloat16)
    store_projected = jnp.zeros((micro_count, row_count, half_value), jnp.bfloat16)
    store_out = jnp.zeros((micro_count, row_count, model_width), jnp.bfloat16)
    arriving = jnp.zeros((row_count, model_width), jnp.bfloat16)
    for step_index in range(step_count):
        micro_index = step_index - section_index
        active = (micro_index >= 0) & (micro_index < micro_count)
        clamped = jnp.clip(micro_index, 0, micro_count - 1)
        entering = jnp.where(section_index == 0, take_slot(slot_hidden, clamped), arriving)
        values, inverse, normed = norm_forward(entering, norm_gain)
        projected = jnp.dot(normed, w_first, preferred_element_type=jnp.float32).astype(
            jnp.bfloat16
        )
        partial_out = jnp.dot(projected, w_second, preferred_element_type=jnp.float32)
        mixed_sum = lax.psum(partial_out.astype(jnp.bfloat16), "tensor").astype(jnp.float32)
        leaving = (values + mixed_sum).astype(jnp.bfloat16)
        store_in = put_slot(store_in, entering, clamped, active)
        store_normed = put_slot(store_normed, normed, clamped, active)
        store_projected = put_slot(store_projected, projected, clamped, active)
        store_out = put_slot(store_out, leaving, clamped, active)
        arriving = from_behind(leaving, "section", 1)
    store_upstream = jnp.zeros((micro_count, row_count, model_width), jnp.bfloat16)
    store_grad_value = jnp.zeros((micro_count, row_count, half_value), jnp.bfloat16)
    arriving = jnp.zeros((row_count, model_width), jnp.bfloat16)
    for step_index in range(step_count):
        micro_index = step_index - (section_count - 1 - section_index)
        active = (micro_index >= 0) & (micro_index < micro_count)
        clamped = jnp.clip(micro_index, 0, micro_count - 1)
        top_rows = take_slot(store_out, clamped).astype(jnp.float32)
        unembed_rows = take_slot(slot_unembed, clamped).astype(jnp.float32)
        logit = jnp.sum(top_rows * unembed_rows, axis=-1)
        seed_rows = take_slot(weight_rows, clamped) * jnp.exp(
            logit - take_slot(logit_base, clamped)
        )
        start_grad = (seed_rows[:, None] * unembed_rows).astype(jnp.bfloat16)
        upstream = jnp.where(is_last, start_grad, arriving)
        entering = take_slot(store_in, clamped)
        normed = take_slot(store_normed, clamped)
        projected = take_slot(store_projected, clamped)
        grad_projected = contract_last(upstream, w_second).astype(jnp.bfloat16)
        partial_norm = contract_last(grad_projected, w_first)
        grad_normed = lax.psum(partial_norm.astype(jnp.bfloat16), "tensor").astype(jnp.float32)
        values, inverse, unused_normed = norm_forward(entering, norm_gain)
        grad_entering = (
            upstream.astype(jnp.float32) + norm_backward(values, inverse, norm_gain, grad_normed)
        ).astype(jnp.bfloat16)
        store_upstream = put_slot(store_upstream, upstream, clamped, active)
        store_grad_value = put_slot(store_grad_value, grad_projected, clamped, active)
        arriving = from_behind(grad_entering, "section", -1)
    flat_normed = store_normed.reshape(micro_count * row_count, model_width)
    flat_upstream = store_upstream.reshape(micro_count * row_count, model_width)
    flat_grad_value = store_grad_value.reshape(micro_count * row_count, half_value)
    flat_projected = store_projected.reshape(micro_count * row_count, half_value)
    reduced = lax.psum_scatter(
        jnp.concatenate(
            [
                contract_first(flat_normed, flat_grad_value),
                contract_first(flat_upstream, flat_projected),
            ],
            axis=1,
        ).astype(jnp.bfloat16),
        "dp",
        scatter_dimension=0,
        tiled=True,
    ).astype(jnp.float32)
    token_total = lax.psum(local_count, "dp")
    scaled_grads = reduced / token_total
    grad_value = scaled_grads[:, :half_value][None]
    grad_output = scaled_grads[:, half_value:].T[None]
    return (grad_value, grad_output)


def solution(mesh):
    placed = (
        P(("groups", "dp"), None, None),
        P(("groups", "dp"), None, None),
        P("section", "dp", "tensor"),
        P("section", "tensor", "dp"),
        P("section", None),
        P(("groups", "dp")),
        P(("groups", "dp")),
        P(("groups", "dp")),
        P(("groups", "dp")),
        P(("groups", "dp"), None),
        P(("groups", "dp"), None),
    )
    return jax.shard_map(
        local,
        mesh=mesh,
        in_specs=placed,
        out_specs=(
            P(("groups", "section"), "dp", "tensor"),
            P(("groups", "section"), "tensor", "dp"),
        ),
        check_vma=False,
    )
```

profile of v0, /device:TPU:0, one launch (start us, length us, event | category | flops | bytes accessed | tf_op | source)
XLA Modules:
  0.0 449.3 jit_solution(629598408572374933)
XLA Ops:
  9.5 1.7 gather_fusion.2
  11.2 1.7 gather_fusion.4
  14.8 2.0 broadcast_select_fusion.1
  18.2 48.9 %all-gather.3.cloned.1.call-done = bf16[1,5120,256]{2,1,0:T(8,128)(2,1)} async-done(((bf16[1,1280,256]{2,1,0:T(8,128)(2,1)}), bf16[1,5120,256]{2,1,0:T(8,128)(2,1)}) %all-gather.3.cloned.1.call-update) | async-done | bytes 2621456 | tf_op jit(solution)/shard_map/all_gather | solution.py:82
  67.1 2.6 bitcast_dynamic-update-slice_fusion.10
  69.7 52.5 %all-gather.5.cloned.1.call-done = bf16[1,256,5120]{2,1,0:T(8,128)(2,1)} async-done(((bf16[1,256,1280]{2,1,0:T(8,128)(2,1)}), bf16[1,256,5120]{2,1,0:T(8,128)(2,1)}) %all-gather.5.cloned.1.call-update) | async-done | bytes 2621456 | tf_op jit(solution)/shard_map/all_gather | solution.py:83
  122.2 3.2 convolution_convert_fusion.4
  125.7 1.2 broadcast.209.clone
  128.5 14.6 %all-reduce.6.cloned.1.call-done = bf16[64,5120]{1,0:T(8,128)(2,1)} async-done(((bf16[64,5120]{1,0:T(8,128)(2,1)}), bf16[64,5120]{1,0:T(8,128)(2,1)}) %all-reduce.6.cloned.1.call-update) | async-done | bytes 655376 | tf_op jit(solution)/shard_map/psum | solution.py:117
  143.2 1.2 copy-done.14
  144.4 1.4 bitcast_dynamic-update-slice_fusion.5
  145.8 3.7 collective-permute-start
  150.7 13.2 %collective-permute-done = bf16[64,5120]{1,0:T(8,128)(2,1)S(1)} collective-permute-done((bf16[64,5120]{1,0:T(8,128)(2,1)S(1)}, bf16[64,5120]{1,0:T(8,128)(2,1)S(1)}, u32[]{:S(2)}, u32[]{:S(2)}) %collective-permute-start) | collective-permute-done | bytes 655392 | tf_op jit(solution)/shard_map/ppermute | solution.py:18
  167.0 1.5 convolution_convert_fusion.3
  168.6 2.0 constant_dynamic-slice_fusion.14
  170.6 2.0 constant_dynamic-slice_fusion.8
  172.6 16.8 %all-reduce.8.cloned.1.call-done = bf16[64,5120]{1,0:T(8,128)(2,1)} async-done(((bf16[64,5120]{1,0:T(8,128)(2,1)}), bf16[64,5120]{1,0:T(8,128)(2,1)}) %all-reduce.8.cloned.1.call-update) | async-done | bytes 655376 | tf_op jit(solution)/shard_map/psum | solution.py:117
  189.4 2.5 bitcast_dynamic-update-slice_fusion.4
  191.9 3.7 collective-permute-start.1
  195.6 2.2 constant_dynamic-slice_fusion.13
  197.8 12.1 %collective-permute-done.1 = bf16[64,5120]{1,0:T(8,128)(2,1)S(1)} collective-permute-done((bf16[64,5120]{1,0:T(8,128)(2,1)S(1)}, bf16[64,5120]{1,0:T(8,128)(2,1)S(1)}, u32[]{:S(2)}, u32[]{:S(2)}) %collective-permute-start.1) | collective-permute-done | bytes 655392 | tf_op jit(solution)/shard_map/ppermute | solution.py:18
  210.1 1.4 bitcast_dynamic-update-slice_fusion.2
  213.9 1.4 convolution_convert_fusion.2
  215.4 1.2 constant_dynamic-slice_fusion.17
  219.3 17.0 %all-reduce.10.cloned.1.call-done = bf16[64,5120]{1,0:T(8,128)(2,1)} async-done(((bf16[64,5120]{1,0:T(8,128)(2,1)}), bf16[64,5120]{1,0:T(8,128)(2,1)}) %all-reduce.10.cloned.1.call-update) | async-done | bytes 655376 | tf_op jit(solution)/shard_map/psum | solution.py:117
  236.2 3.1 bitcast_dynamic-update-slice_fusion.6
  239.3 2.4 fusion.32
  243.5 1.7 convolution_convert_fusion.1
  247.6 17.8 %all-reduce.12.cloned.1.call-done = bf16[64,5120]{1,0:T(8,128)(2,1)} async-done(((bf16[64,5120]{1,0:T(8,128)(2,1)}), bf16[64,5120]{1,0:T(8,128)(2,1)}) %all-reduce.12.cloned.1.call-update) | async-done | bytes 655376 | tf_op jit(solution)/shard_map/psum | solution.py:144
  265.4 2.1 fusion.48
  267.6 1.6 fusion.46
  269.2 1.5 collective-permute-start.2
  271.8 16.1 %collective-permute-done.2 = bf16[64,5120]{1,0:T(8,128)(2,1)S(1)} collective-permute-done((bf16[64,5120]{1,0:T(8,128)(2,1)S(1)}, bf16[64,5120]{1,0:T(8,128)(2,1)S(1)}, u32[]{:S(2)}, u32[]{:S(2)}) %collective-permute-start.2) | collective-permute-done | bytes 655392 | tf_op jit(solution)/shard_map/ppermute | solution.py:18
  288.0 1.2 bitcast_dynamic-update-slice_fusion.1
  291.7 1.7 convolution_convert_fusion
  293.5 19.2 %all-reduce.14.cloned.1.call-done = bf16[64,5120]{1,0:T(8,128)(2,1)} async-done(((bf16[64,5120]{1,0:T(8,128)(2,1)}), bf16[64,5120]{1,0:T(8,128)(2,1)}) %all-reduce.14.cloned.1.call-update) | async-done | bytes 655376 | tf_op jit(solution)/shard_map/psum | solution.py:144
  312.7 1.7 fusion.53
  314.4 1.7 fusion.52
  316.1 1.3 collective-permute-start.3
  318.6 16.3 %collective-permute-done.3 = bf16[64,5120]{1,0:T(8,128)(2,1)S(1)} collective-permute-done((bf16[64,5120]{1,0:T(8,128)(2,1)S(1)}, bf16[64,5120]{1,0:T(8,128)(2,1)S(1)}, u32[]{:S(2)}, u32[]{:S(2)}) %collective-permute-start.3) | collective-permute-done | bytes 655392 | tf_op jit(solution)/shard_map/ppermute | solution.py:18
  337.1 1.2 bitcast_dynamic-update-slice_fusion
  338.3 2.2 fusion.1
  340.5 2.7 pad_maximum_fusion
  344.5 12.9 %psum.47 = f32[]{:T(128)} all-reduce(f32[]{:T(128)} %convert_reduce_fusion), channel_id=1, replica_groups=mesh['groups'=2,'dp'=4,'section'=2,'tensor'=2] {'dp'}, use_global_device_ids=true, to_apply=%region_17.20 | all-reduce | flops 1 | bytes 8 | tf_op jit(solution)/shard_map/psum | solution.py:168
  357.4 80.2 %reduce-scatter.2.cloned.1.call-done = bf16[1280,512]{0,1:T(8,128)(2,1)} async-done(((bf16[5120,512]{0,1:T(8,128)(2,1)}), bf16[1280,512]{0,1:T(8,128)(2,1)}) %reduce-scatter.2.cloned.1.call-update) | async-done | bytes 1310736 | tf_op jit(solution)/shard_map/reduce_scatter | solution.py:156
  437.6 2.2 convert_divide_fusion
  439.7 1.2 slice_bitcast_fusion
  441.0 1.5 copy.18
  (126 shorter events, 28.8 us)
Async XLA Ops:
  7.2 2.3 copy-start
  7.2 1.6 copy-start.30
  7.2 1.6 copy-start.1
  7.2 59.9 %all-gather.3.cloned.1.call-start = ((), (), s32[]{:S(2)}) async-start(), calls=%async_computation.1 | async-start | bytes 3276800 | tf_op jit(solution)/shard_map/all_gather | solution.py:82
  7.9 114.3 %all-gather.5.cloned.1.call-start = ((), (), s32[]{:S(2)}) async-start(), calls=%async_computation.2 | async-start | bytes 3276800 | tf_op jit(solution)/shard_map/all_gather | solution.py:83
  8.7 134.4 %all-reduce.6.cloned.1.call-start = ((), (), s32[]{:S(2)}) async-start(), calls=%async_computation.3 | async-start | bytes 1310720 | tf_op jit(solution)/shard_map/psum | solution.py:117
  9.5 1.7 copy-start.27
  11.2 1.7 copy-start.2
  11.2 2.4 copy-start.28
  11.2 3.0 copy-start.29
  14.8 52.3 %copy-start.26 = (f32[1,5120]{1,0:T(1,128)S(1)}, f32[1,5120]{1,0:T(1,128)}, u32[]{:S(2)}) copy-start(f32[1,5120]{1,0:T(1,128)} %param.19) | copy-start | bytes 61444
  16.8 1.1 copy-start.12
  125.4 64.0 %all-reduce.8.cloned.1.call-start = ((), (), s32[]{:S(2)}) async-start(), calls=%async_computation.4 | async-start | bytes 1310720 | tf_op jit(solution)/shard_map/psum | solution.py:117
  125.7 1.8 copy-start.13
  143.1 1.3 copy-start.14
  145.8 4.9 %copy-start.20 = (bf16[2,64,5120]{2,1,0:T(8,128)(2,1)}, bf16[2,64,5120]{2,1,0:T(8,128)(2,1)S(1)}, u32[]{:S(2)}) copy-start(bf16[2,64,5120]{2,1,0:T(8,128)(2,1)S(1)} %get-tuple-element.22) | copy-start | bytes 3932164
  145.8 18.1 %collective-permute-start = (bf16[64,5120]{1,0:T(8,128)(2,1)S(1)}, bf16[64,5120]{1,0:T(8,128)(2,1)S(1)}, u32[]{:S(2)}, u32[]{:S(2)}) collective-permute-start(bf16[64,5120]{1,0:T(8,128)(2,1)S(1)} %get-tuple-element.23), channel_id=1, source_target_pairs={{0,2},{1,3},{4,6},{5,7},{8,10},{9,11},{12,14},{13,15},{16,18},{17,... | collective-permute-start | bytes 1966088 | tf_op jit(solution)/shard_map/ppermute | solution.py:18
  150.7 14.6 %copy-start.8 = (bf16[1,5120,256]{2,1,0:T(8,128)(2,1)S(1)}, bf16[1,5120,256]{2,1,0:T(8,128)(2,1)}, u32[]{:S(2)}) copy-start(bf16[1,5120,256]{2,1,0:T(8,128)(2,1)} %all-gather.3.cloned.1.call-done) | copy-start | bytes 7864324
  165.3 1.7 copy-start.3
  168.5 67.7 %all-reduce.10.cloned.1.call-start = ((), (), s32[]{:S(2)}) async-start(), calls=%async_computation.5 | async-start | bytes 1310720 | tf_op jit(solution)/shard_map/psum | solution.py:117
  191.9 18.1 %collective-permute-start.1 = (bf16[64,5120]{1,0:T(8,128)(2,1)S(1)}, bf16[64,5120]{1,0:T(8,128)(2,1)S(1)}, u32[]{:S(2)}, u32[]{:S(2)}) collective-permute-start(bf16[64,5120]{1,0:T(8,128)(2,1)S(1)} %get-tuple-element.21), channel_id=1, source_target_pairs={{0,2},{1,3},{4,6},{5,7},{8,10},{9,11},{12,14},{13,15},{16,18},{17,... | collective-permute-start | bytes 1966088 | tf_op jit(solution)/shard_map/ppermute | solution.py:18
  195.6 14.5 %copy-start.15 = (bf16[16,8,5120]{2,1,0:T(8,128)(2,1)S(1)}, bf16[16,8,5120]{2,1,0:T(8,128)(2,1)}, u32[]{:S(2)}) copy-start(bf16[16,8,5120]{2,1,0:T(8,128)(2,1)} %copy-done.12) | copy-start | bytes 3932164
  195.6 14.5 %copy-start.25 = (bf16[1,64,5120]{2,1,0:T(8,128)(2,1)S(1)}, bf16[1,64,5120]{2,1,0:T(8,128)(2,1)}, u32[]{:S(2)}) copy-start(bf16[1,64,5120]{2,1,0:T(8,128)(2,1)} %constant_dynamic-slice_fusion.8) | copy-start | bytes 1966084
  210.1 2.0 copy-start.9
  211.5 1.2 copy-start.16
  211.5 1.3 copy-start.21
  212.0 1.9 copy-start.4
  215.4 50.0 %all-reduce.12.cloned.1.call-start = ((), (), s32[]{:S(2)}) async-start(), calls=%async_computation.6 | async-start | bytes 1310720 | tf_op jit(solution)/shard_map/psum | solution.py:144
  215.4 1.5 copy-start.17
  217.3 1.1 copy-start.18
  218.4 17.8 %copy-start.22 = (bf16[64,5120]{1,0:T(8,128)(2,1)S(1)}, bf16[64,5120]{1,0:T(8,128)(2,1)}, u32[]{:S(2)}) copy-start(bf16[64,5120]{1,0:T(8,128)(2,1)} %copy-done.21) | copy-start | bytes 1966084
  239.3 2.4 copy-start.5
  241.8 1.7 copy-start.10
  245.3 67.4 %all-reduce.14.cloned.1.call-start = ((), (), s32[]{:S(2)}) async-start(), calls=%async_computation.7 | async-start | bytes 1310720 | tf_op jit(solution)/shard_map/psum | solution.py:144
  265.4 2.1 copy-start.24
  269.2 18.8 %collective-permute-start.2 = (bf16[64,5120]{1,0:T(8,128)(2,1)S(1)}, bf16[64,5120]{1,0:T(8,128)(2,1)S(1)}, u32[]{:S(2)}, u32[]{:S(2)}) collective-permute-start(bf16[64,5120]{1,0:T(8,128)(2,1)S(1)} %fusion.46), channel_id=1, source_target_pairs={{2,0},{3,1},{6,4},{7,5},{10,8},{11,9},{14,12},{15,13},{18,16},{19,... | collective-permute-start | bytes 1966088 | tf_op jit(solution)/shard_map/ppermute | solution.py:18
  288.0 2.0 copy-start.6
  290.0 1.7 copy-start.11
  293.5 144.1 %reduce-scatter.2.cloned.1.call-start = ((), (), s32[]{:S(2)}) async-start(), calls=%async_computation.8 | async-start | bytes 6553600 | tf_op jit(solution)/shard_map/reduce_scatter | solution.py:156
  312.7 1.7 copy-start.23
  314.4 20.5 %copy-start.7 = (bf16[1,256,5120]{2,1,0:T(8,128)(2,1)S(1)}, bf16[1,256,5120]{2,1,0:T(8,128)(2,1)}, u32[]{:S(2)}) copy-start(bf16[1,256,5120]{2,1,0:T(8,128)(2,1)} %all-gather.5.cloned.1.call-done) | copy-start | bytes 7864324
  316.1 18.8 %collective-permute-start.3 = (bf16[64,5120]{1,0:T(8,128)(2,1)S(1)}, bf16[64,5120]{1,0:T(8,128)(2,1)S(1)}, u32[]{:S(2)}, u32[]{:S(2)}) collective-permute-start(bf16[64,5120]{1,0:T(8,128)(2,1)S(1)} %fusion.52), channel_id=1, source_target_pairs={{2,0},{3,1},{6,4},{7,5},{10,8},{11,9},{14,12},{15,13},{18,16},{19,... | collective-permute-start | bytes 1966088 | tf_op jit(solution)/shard_map/ppermute | solution.py:18
  334.9 1.3 copy-start.19
Sparse Core Ops, SparseCore 0:
  9.6 57.4 all-gather.2
  68.6 53.4 all-gather.4
  125.5 17.5 all-reduce.5
  168.6 20.6 all-reduce.7
  215.5 20.6 all-reduce.9
  245.4 19.9 all-reduce.11
  293.6 19.0 all-reduce.13
  343.3 94.1 reduce-scatter.1
where the time goes:
time: 450 us; the launch traced here: 449 us
  waiting for transfers between devices  326 us (72%)
  local copies, waits for them, and re-layouts  32.9 us (7%)
  other arithmetic  32.2 us (7%)
  matrix products  19.3 us (4%)
  between operations  15.3 us (3%)
  blocking collectives  12.9 us (3%)
  starting transfers between devices  10.5 us (2%)
    reduce_scatter x1, waiting for transfers between devices, local(): lax.psum_scatter(jnp.concatenate([contract_first(flat_normed, flat_grad_v...  80.2 us
    ppermute x4, waiting for transfers between devices, from_behind(): return lax.ppermute(block, axis, route)  57.8 us
    all_gather x1, waiting for transfers between devices, local(): lax.all_gather(output_proj, 'dp', axis=2, tiled=True)  52.5 us
    all_gather x1, waiting for transfers between devices, local(): lax.all_gather(value_proj, 'dp', axis=1, tiled=True)  48.9 us
    psum x3, waiting for transfers between devices, local(): lax.psum(partial_out.astype(jnp.bfloat16), 'tensor').astype(jnp.float32)  48.4 us
    psum x2, waiting for transfers between devices, local(): lax.psum(partial_norm.astype(jnp.bfloat16), 'tensor').astype(jnp.float32)  37 us
    dynamic_update_slice x10, other arithmetic, put_slot(): lax.dynamic_update_index_in_dim(slot_store, jnp.where(active, new_value,...  14.3 us
    psum x1, blocking collectives, local(): token_total = lax.psum(local_count, 'dp')  12.9 us
  transfers between devices with their start and end apart: 12, of which 12 were waited for; matrix products, arithmetic and copies ran while one was open for 6% of the time, Pallas kernels for 0%

commit v1 on v0

--- a/solution.py
+++ b/solution.py
@@ -141,7 +141,9 @@
         projected = take_slot(store_projected, clamped)
         grad_projected = contract_last(upstream, w_second).astype(jnp.bfloat16)
         partial_norm = contract_last(grad_projected, w_first)
-        grad_normed = lax.psum(partial_norm.astype(jnp.bfloat16), "tensor").astype(jnp.float32)
+        grad_normed = jnp.sum(
+            lax.all_gather(partial_norm.astype(jnp.bfloat16), "tensor"), axis=0
+        ).astype(jnp.float32)
         values, inverse, unused_normed = norm_forward(entering, norm_gain)
         grad_entering = (
             upstream.astype(jnp.float32) + norm_backward(values, inverse, norm_gain, grad_normed)

time: 450 us -> 435 us (0.967)
  waiting for transfers between devices: 326 us -> 307 us
    psum x2 -> x0, waiting for transfers between devices: 37 us -> none  [local(): lax.psum(partial_norm.astype(jnp.bfloat16), 'tensor').astype(jnp.float32)]
    all_gather x0 -> x2, waiting for transfers between devices: none -> 18.3 us  [local(): lax.all_gather(partial_norm.astype(jnp.bfloat16), 'tensor')]
  transfers between devices with their start and end apart: 12 -> 12, of which waited for: 12 -> 12; matrix products, arithmetic and copies ran while one was open for 6% -> 7% of each run, Pallas kernels for 0% -> 0%
where the time goes in v1:
time: 435 us; the launch traced here: 433 us
  waiting for transfers between devices  307 us (71%)
  other arithmetic  35 us (8%)
  local copies, waits for them, and re-layouts  32.9 us (8%)
  matrix products  19.3 us (4%)
  between operations  15.3 us (4%)
  blocking collectives  13 us (3%)
  starting transfers between devices  10.5 us (2%)
    reduce_scatter x1, waiting for transfers between devices, local(): lax.psum_scatter(jnp.concatenate([contract_first(flat_normed, flat_grad_v...  80.2 us
    ppermute x4, waiting for transfers between devices, from_behind(): return lax.ppermute(block, axis, route)  57.7 us
    all_gather x1, waiting for transfers between devices, local(): lax.all_gather(output_proj, 'dp', axis=2, tiled=True)  52.5 us
    all_gather x1, waiting for transfers between devices, local(): lax.all_gather(value_proj, 'dp', axis=1, tiled=True)  48.9 us
    psum x3, waiting for transfers between devices, local(): lax.psum(partial_out.astype(jnp.bfloat16), 'tensor').astype(jnp.float32)  48.4 us
    all_gather x2, waiting for transfers between devices, local(): lax.all_gather(partial_norm.astype(jnp.bfloat16), 'tensor')  18.3 us
    dynamic_update_slice x10, other arithmetic, put_slot(): lax.dynamic_update_index_in_dim(slot_store, jnp.where(active, new_value,...  14.3 us
    psum x1, blocking collectives, local(): token_total = lax.psum(local_count, 'dp')  13 us
  transfers between devices with their start and end apart: 12, of which 12 were waited for; matrix products, arithmetic and copies ran while one was open for 7% of the time, Pallas kernels for 0%

profile of v1, /device:TPU:0, one launch (start us, length us, event | category | flops | bytes accessed | tf_op | source)
XLA Modules:
  0.0 433.4 jit_solution(9999579876278382536)
XLA Ops:
  9.5 1.7 gather_fusion.2
  11.2 1.7 gather_fusion.4
  14.8 2.0 broadcast_select_fusion.1
  18.2 48.9 %all-gather.7.cloned.1.call-done = bf16[1,5120,256]{2,1,0:T(8,128)(2,1)} async-done(((bf16[1,1280,256]{2,1,0:T(8,128)(2,1)}), bf16[1,5120,256]{2,1,0:T(8,128)(2,1)}) %all-gather.7.cloned.1.call-update) | async-done | bytes 2621456 | tf_op jit(solution)/shard_map/all_gather | solution.py:82
  67.1 2.6 bitcast_dynamic-update-slice_fusion.10
  69.7 52.5 %all-gather.9.cloned.1.call-done = bf16[1,256,5120]{2,1,0:T(8,128)(2,1)} async-done(((bf16[1,256,1280]{2,1,0:T(8,128)(2,1)}), bf16[1,256,5120]{2,1,0:T(8,128)(2,1)}) %all-gather.9.cloned.1.call-update) | async-done | bytes 2621456 | tf_op jit(solution)/shard_map/all_gather | solution.py:83
  122.2 3.2 convolution_convert_fusion.4
  125.7 1.2 broadcast.209.clone
  128.5 14.6 %all-reduce.4.cloned.1.call-done = bf16[64,5120]{1,0:T(8,128)(2,1)} async-done(((bf16[64,5120]{1,0:T(8,128)(2,1)}), bf16[64,5120]{1,0:T(8,128)(2,1)}) %all-reduce.4.cloned.1.call-update) | async-done | bytes 655376 | tf_op jit(solution)/shard_map/psum | solution.py:117
  144.4 1.4 bitcast_dynamic-update-slice_fusion.5
  145.8 3.7 collective-permute-start
  150.7 13.2 %collective-permute-done = bf16[64,5120]{1,0:T(8,128)(2,1)S(1)} collective-permute-done((bf16[64,5120]{1,0:T(8,128)(2,1)S(1)}, bf16[64,5120]{1,0:T(8,128)(2,1)S(1)}, u32[]{:S(2)}, u32[]{:S(2)}) %collective-permute-start) | collective-permute-done | bytes 655392 | tf_op jit(solution)/shard_map/ppermute | solution.py:18
  167.0 1.5 convolution_convert_fusion.3
  168.6 2.0 constant_dynamic-slice_fusion.14
  170.6 2.0 constant_dynamic-slice_fusion.8
  172.6 16.8 %all-reduce.6.cloned.1.call-done = bf16[64,5120]{1,0:T(8,128)(2,1)} async-done(((bf16[64,5120]{1,0:T(8,128)(2,1)}), bf16[64,5120]{1,0:T(8,128)(2,1)}) %all-reduce.6.cloned.1.call-update) | async-done | bytes 655376 | tf_op jit(solution)/shard_map/psum | solution.py:117
  189.4 2.5 bitcast_dynamic-update-slice_fusion.4
  191.9 3.7 collective-permute-start.1
  195.6 2.2 constant_dynamic-slice_fusion.13
  197.8 12.1 %collective-permute-done.1 = bf16[64,5120]{1,0:T(8,128)(2,1)S(1)} collective-permute-done((bf16[64,5120]{1,0:T(8,128)(2,1)S(1)}, bf16[64,5120]{1,0:T(8,128)(2,1)S(1)}, u32[]{:S(2)}, u32[]{:S(2)}) %collective-permute-start.1) | collective-permute-done | bytes 655392 | tf_op jit(solution)/shard_map/ppermute | solution.py:18
  210.1 1.4 bitcast_dynamic-update-slice_fusion.2
  213.9 1.4 convolution_convert_fusion.2
  215.4 1.2 constant_dynamic-slice_fusion.17
  219.3 17.0 %all-reduce.8.cloned.1.call-done = bf16[64,5120]{1,0:T(8,128)(2,1)} async-done(((bf16[64,5120]{1,0:T(8,128)(2,1)}), bf16[64,5120]{1,0:T(8,128)(2,1)}) %all-reduce.8.cloned.1.call-update) | async-done | bytes 655376 | tf_op jit(solution)/shard_map/psum | solution.py:117
  236.2 3.1 bitcast_dynamic-update-slice_fusion.6
  239.3 2.4 fusion.32
  243.5 1.8 convolution_convert_fusion.1
  247.7 8.4 %all-gather.11.cloned.1.call-done = bf16[128,5120]{1,0:T(8,128)(2,1)} async-done(((bf16[64,5120]{1,0:T(8,128)(2,1)}), bf16[128,5120]{1,0:T(8,128)(2,1)}) %all-gather.11.cloned.1.call-update) | async-done | bytes 1310736 | tf_op jit(solution)/shard_map/all_gather | solution.py:145
  256.1 1.6 reduce_sum.129
  257.7 1.9 fusion.48
  259.6 1.6 fusion.46
  261.3 1.5 collective-permute-start.2
  263.9 16.1 %collective-permute-done.2 = bf16[64,5120]{1,0:T(8,128)(2,1)S(1)} collective-permute-done((bf16[64,5120]{1,0:T(8,128)(2,1)S(1)}, bf16[64,5120]{1,0:T(8,128)(2,1)S(1)}, u32[]{:S(2)}, u32[]{:S(2)}) %collective-permute-start.2) | collective-permute-done | bytes 655392 | tf_op jit(solution)/shard_map/ppermute | solution.py:18
  280.0 1.2 bitcast_dynamic-update-slice_fusion.1
  283.7 1.8 convolution_convert_fusion
  285.6 9.8 %all-gather.13.cloned.1.call-done = bf16[128,5120]{1,0:T(8,128)(2,1)} async-done(((bf16[64,5120]{1,0:T(8,128)(2,1)}), bf16[128,5120]{1,0:T(8,128)(2,1)}) %all-gather.13.cloned.1.call-update) | async-done | bytes 1310736 | tf_op jit(solution)/shard_map/all_gather | solution.py:145
  295.4 1.6 reduce_sum.133
  297.0 1.5 fusion.53
  298.6 1.7 fusion.52
  300.3 1.3 collective-permute-start.3
  302.7 16.3 %collective-permute-done.3 = bf16[64,5120]{1,0:T(8,128)(2,1)S(1)} collective-permute-done((bf16[64,5120]{1,0:T(8,128)(2,1)S(1)}, bf16[64,5120]{1,0:T(8,128)(2,1)S(1)}, u32[]{:S(2)}, u32[]{:S(2)}) %collective-permute-start.3) | collective-permute-done | bytes 655392 | tf_op jit(solution)/shard_map/ppermute | solution.py:18
  322.4 2.2 fusion.1
  324.6 2.7 pad_maximum_fusion
  328.6 13.0 %psum.31 = f32[]{:T(128)} all-reduce(f32[]{:T(128)} %convert_reduce_fusion), channel_id=1, replica_groups=mesh['groups'=2,'dp'=4,'section'=2,'tensor'=2] {'dp'}, use_global_device_ids=true, to_apply=%region_17.20 | all-reduce | flops 1 | bytes 8 | tf_op jit(solution)/shard_map/psum | solution.py:170
  341.6 80.2 %reduce-scatter.2.cloned.1.call-done = bf16[1280,512]{0,1:T(8,128)(2,1)} async-done(((bf16[5120,512]{0,1:T(8,128)(2,1)}), bf16[1280,512]{0,1:T(8,128)(2,1)}) %reduce-scatter.2.cloned.1.call-update) | async-done | bytes 1310736 | tf_op jit(solution)/shard_map/reduce_scatter | solution.py:158
  421.7 2.2 convert_divide_fusion
  423.9 1.2 slice_bitcast_fusion
  425.1 1.5 copy.18
  (128 shorter events, 31.2 us)
Async XLA Ops:
  7.2 2.3 copy-start
  7.2 1.6 copy-start.30
  7.2 1.6 copy-start.1
  7.2 59.9 %all-gather.7.cloned.1.call-start = ((), (), s32[]{:S(2)}) async-start(), calls=%async_computation.1 | async-start | bytes 3276800 | tf_op jit(solution)/shard_map/all_gather | solution.py:82
  7.9 114.3 %all-gather.9.cloned.1.call-start = ((), (), s32[]{:S(2)}) async-start(), calls=%async_computation.2 | async-start | bytes 3276800 | tf_op jit(solution)/shard_map/all_gather | solution.py:83
  8.7 134.4 %all-reduce.4.cloned.1.call-start = ((), (), s32[]{:S(2)}) async-start(), calls=%async_computation.3 | async-start | bytes 1310720 | tf_op jit(solution)/shard_map/psum | solution.py:117
  9.5 1.7 copy-start.27
  11.2 1.7 copy-start.2
  11.2 2.4 copy-start.28
  11.2 3.0 copy-start.29
  14.8 52.3 %copy-start.26 = (f32[1,5120]{1,0:T(1,128)S(1)}, f32[1,5120]{1,0:T(1,128)}, u32[]{:S(2)}) copy-start(f32[1,5120]{1,0:T(1,128)} %param.19) | copy-start | bytes 61444
  16.8 1.1 copy-start.12
  125.4 64.0 %all-reduce.6.cloned.1.call-start = ((), (), s32[]{:S(2)}) async-start(), calls=%async_computation.4 | async-start | bytes 1310720 | tf_op jit(solution)/shard_map/psum | solution.py:117
  125.7 1.8 copy-start.13
  143.1 1.3 copy-start.14
  145.8 4.9 %copy-start.20 = (bf16[2,64,5120]{2,1,0:T(8,128)(2,1)}, bf16[2,64,5120]{2,1,0:T(8,128)(2,1)S(1)}, u32[]{:S(2)}) copy-start(bf16[2,64,5120]{2,1,0:T(8,128)(2,1)S(1)} %get-tuple-element.22) | copy-start | bytes 3932164
  145.8 18.1 %collective-permute-start = (bf16[64,5120]{1,0:T(8,128)(2,1)S(1)}, bf16[64,5120]{1,0:T(8,128)(2,1)S(1)}, u32[]{:S(2)}, u32[]{:S(2)}) collective-permute-start(bf16[64,5120]{1,0:T(8,128)(2,1)S(1)} %get-tuple-element.23), channel_id=1, source_target_pairs={{0,2},{1,3},{4,6},{5,7},{8,10},{9,11},{12,14},{13,15},{16,18},{17,... | collective-permute-start | bytes 1966088 | tf_op jit(solution)/shard_map/ppermute | solution.py:18
  150.7 14.6 %copy-start.8 = (bf16[1,5120,256]{2,1,0:T(8,128)(2,1)S(1)}, bf16[1,5120,256]{2,1,0:T(8,128)(2,1)}, u32[]{:S(2)}) copy-start(bf16[1,5120,256]{2,1,0:T(8,128)(2,1)} %all-gather.7.cloned.1.call-done) | copy-start | bytes 7864324
  165.3 1.7 copy-start.3
  168.5 67.7 %all-reduce.8.cloned.1.call-start = ((), (), s32[]{:S(2)}) async-start(), calls=%async_computation.5 | async-start | bytes 1310720 | tf_op jit(solution)/shard_map/psum | solution.py:117
  191.9 18.1 %collective-permute-start.1 = (bf16[64,5120]{1,0:T(8,128)(2,1)S(1)}, bf16[64,5120]{1,0:T(8,128)(2,1)S(1)}, u32[]{:S(2)}, u32[]{:S(2)}) collective-permute-start(bf16[64,5120]{1,0:T(8,128)(2,1)S(1)} %get-tuple-element.21), channel_id=1, source_target_pairs={{0,2},{1,3},{4,6},{5,7},{8,10},{9,11},{12,14},{13,15},{16,18},{17,... | collective-permute-start | bytes 1966088 | tf_op jit(solution)/shard_map/ppermute | solution.py:18
  195.6 14.5 %copy-start.15 = (bf16[16,8,5120]{2,1,0:T(8,128)(2,1)S(1)}, bf16[16,8,5120]{2,1,0:T(8,128)(2,1)}, u32[]{:S(2)}) copy-start(bf16[16,8,5120]{2,1,0:T(8,128)(2,1)} %copy-done.12) | copy-start | bytes 3932164
  195.6 14.5 %copy-start.25 = (bf16[1,64,5120]{2,1,0:T(8,128)(2,1)S(1)}, bf16[1,64,5120]{2,1,0:T(8,128)(2,1)}, u32[]{:S(2)}) copy-start(bf16[1,64,5120]{2,1,0:T(8,128)(2,1)} %constant_dynamic-slice_fusion.8) | copy-start | bytes 1966084
  210.1 2.0 copy-start.9
  211.5 1.2 copy-start.16
  211.5 1.3 copy-start.21
  212.0 1.9 copy-start.4
  215.4 40.7 %all-gather.11.cloned.1.call-start = ((), (), s32[]{:S(2)}) async-start(), calls=%async_computation.7 | async-start | bytes 1966080 | tf_op jit(solution)/shard_map/all_gather | solution.py:145
  215.4 1.5 copy-start.17
  217.3 1.1 copy-start.18
  218.4 17.8 %copy-start.22 = (bf16[64,5120]{1,0:T(8,128)(2,1)S(1)}, bf16[64,5120]{1,0:T(8,128)(2,1)}, u32[]{:S(2)}) copy-start(bf16[64,5120]{1,0:T(8,128)(2,1)} %copy-done.21) | copy-start | bytes 1966084
  239.3 2.4 copy-start.5
  241.8 1.7 copy-start.10
  245.3 50.1 %all-gather.13.cloned.1.call-start = ((), (), s32[]{:S(2)}) async-start(), calls=%async_computation.8 | async-start | bytes 1966080 | tf_op jit(solution)/shard_map/all_gather | solution.py:145
  261.3 18.8 %collective-permute-start.2 = (bf16[64,5120]{1,0:T(8,128)(2,1)S(1)}, bf16[64,5120]{1,0:T(8,128)(2,1)S(1)}, u32[]{:S(2)}, u32[]{:S(2)}) collective-permute-start(bf16[64,5120]{1,0:T(8,128)(2,1)S(1)} %fusion.46), channel_id=1, source_target_pairs={{2,0},{3,1},{6,4},{7,5},{10,8},{11,9},{14,12},{15,13},{18,16},{19,... | collective-permute-start | bytes 1966088 | tf_op jit(solution)/shard_map/ppermute | solution.py:18
  280.0 2.0 copy-start.6
  281.2 1.7 copy-start.23
  282.0 1.7 copy-start.11
  285.5 136.2 %reduce-scatter.2.cloned.1.call-start = ((), (), s32[]{:S(2)}) async-start(), calls=%async_computation.6 | async-start | bytes 6553600 | tf_op jit(solution)/shard_map/reduce_scatter | solution.py:158
  297.0 1.5 copy-start.24
  298.5 20.5 %copy-start.7 = (bf16[1,256,5120]{2,1,0:T(8,128)(2,1)S(1)}, bf16[1,256,5120]{2,1,0:T(8,128)(2,1)}, u32[]{:S(2)}) copy-start(bf16[1,256,5120]{2,1,0:T(8,128)(2,1)} %all-gather.9.cloned.1.call-done) | copy-start | bytes 7864324
  300.3 18.8 %collective-permute-start.3 = (bf16[64,5120]{1,0:T(8,128)(2,1)S(1)}, bf16[64,5120]{1,0:T(8,128)(2,1)S(1)}, u32[]{:S(2)}, u32[]{:S(2)}) collective-permute-start(bf16[64,5120]{1,0:T(8,128)(2,1)S(1)} %fusion.52), channel_id=1, source_target_pairs={{2,0},{3,1},{6,4},{7,5},{10,8},{11,9},{14,12},{15,13},{18,16},{19,... | collective-permute-start | bytes 1966088 | tf_op jit(solution)/shard_map/ppermute | solution.py:18
  319.0 1.3 copy-start.19
Sparse Core Ops, SparseCore 0:
  9.6 57.4 all-gather.6
  68.6 53.4 all-gather.8
  125.5 17.5 all-reduce.3
  168.6 20.6 all-reduce.5
  215.5 20.6 all-reduce.7
  245.5 10.6 all-gather.10
  285.6 9.7 all-gather.12
  327.4 94.2 reduce-scatter.1
